TPU v7x, 32 devices: a whole 2x2x4 slice. The times are simulated.
32 devices in a mesh: groups: 2 (over y), gx: 4 (over z), gy: 2 (over x), gz: 2 (over core).
Axes of the slice: x: 2, y: 2, z: 4, core: 2. Of those that a mesh axis runs over, the one named last changes fastest.
Arguments:
- latents: bfloat16 [8, 2, 2, 128, 128], P(('groups', 'gx'), 'gy', 'gz'), parts along dimension 0, may hold values from -6 to 6
- offsets: bfloat16 [8, 2, 2, 3, 128], P(('groups', 'gx'), 'gy', 'gz'), parts along dimension 0, may hold values from 0 to 1
- neighbours: int32 [8, 2, 2, 384], P(('groups', 'gx'), 'gy', 'gz'), parts along dimension 0, may hold values from 0 to 2047, as said below
- counts: int32 [8, 2, 2], P(('groups', 'gx'), 'gy', 'gz'), parts along dimension 0, may hold values from 1 to 384, as said below
- w_recv: bfloat16 [1, 128, 128], replicated, may hold values from -0.5 to 0.5
- w_send: bfloat16 [1, 128, 128], replicated, may hold values from -0.5 to 0.5
- w_rel: bfloat16 [1, 4, 128], replicated, may hold values from -3 to 3
- b_first: float32 [1, 128], replicated, may hold values from -5 to 5
- w_edge: bfloat16 [1, 128, 128], replicated, may hold values from -0.5 to 0.5
- b_edge: float32 [1, 128], replicated, may hold values from -5 to 5
- w_self: bfloat16 [1, 128, 128], replicated, may hold values from -0.5 to 0.5
- w_agg: bfloat16 [1, 128, 128], replicated, may hold values from -0.5 to 0.5
- w_out: bfloat16 [1, 128, 128], replicated, may hold values from -0.5 to 0.5
- norm_gain: float32 [1, 128], replicated, may hold values from 0.1 to 1.9
Outputs:
- processed: bfloat16 [8, 2, 2, 128, 128], P(('groups', 'gx'), 'gy', 'gz'), parts along dimension 0
There are 2 independent parts, one for each index of `groups`. A program takes and returns all parts, laid end to end along the dimension named above; an argument that names none is the same for every part. Nothing has to cross between parts.
Inputs may be any that keep to these rules, and one draw needn't show every extreme that they name: `neighbours`: each sender is a particle of the same cell or of a cell whose three coordinates differ from the receiver cell's by at most one. Only the first counts[cell] senders of a cell are live, the rest is padding. In the cells whose first coordinate is below 1 all 384 senders are live.
All inputs are finite; a program needn't handle non-finite values.
Results may differ from a plain program's by a relative error of at most 0.0055.
Values may be sent and summed in bfloat16 or wider, within the bound.
A program may use at most 64 MiB of HBM per device.

v0:
```python
import jax
import jax.numpy as jnp
from jax import lax
from jax.sharding import PartitionSpec as P

SLOTS = 128


def extended(shard, sides, width):
    for axis, dim in sides:
        size, length = (lax.axis_size(axis), shard.shape[dim])
        up = [(i, (i + 1) % size) for i in range(size - 1)]
        down = [(j, i) for i, j in up]
        last = lax.slice_in_dim(shard, length - width, length, axis=dim)
        first = lax.slice_in_dim(shard, 0, width, axis=dim)
        before = lax.ppermute(last, axis, up)
        after = lax.ppermute(first, axis, down)
        shard = jnp.concatenate([before, shard, after], axis=dim)
    return shard


def edge_sum(recv_term, send_term, recv_place, send_place, live_mask, rel_weight, w_edge, b_edge):
    row_count, latent_width = recv_term.shape
    tile_rows = min(16, row_count)
    tile_count = row_count // tile_rows

    def tile_messages(operands):
        recv_tile, place_tile = operands
        relative = send_place[:, None, :] - place_tile[:, :, None]
        features = jnp.concatenate(
            [relative, 0.25 * jnp.sum(relative * relative, axis=0, keepdims=True)], axis=0
        )
        place_term = jnp.einsum(
            "cij,cw->ijw", features, rel_weight, precision=lax.Precision.HIGHEST
        )
        pre_act = recv_tile[:, None, :] + send_term[None, :, :] + place_term
        edge_act = jax.nn.silu(pre_act).astype(jnp.bfloat16)
        message = (
            jnp.dot(edge_act.reshape(-1, latent_width), w_edge, preferred_element_type=jnp.float32)
            + b_edge
        )
        message = jax.nn.silu(message).reshape(tile_rows, -1, latent_width)
        return jnp.einsum("ijw,j->iw", message, live_mask, precision=lax.Precision.HIGHEST)

    recv_tiles = recv_term.reshape(tile_count, tile_rows, latent_width)
    place_tiles = recv_place.reshape(3, tile_count, tile_rows).transpose(1, 0, 2)
    return lax.map(tile_messages, (recv_tiles, place_tiles)).reshape(row_count, latent_width)


def renew(latent, summed, w_self, w_agg, w_out, norm_gain):
    pooled = (summed / latent.shape[0]).astype(jnp.bfloat16)
    hidden = jax.nn.silu(
        jnp.dot(latent, w_self, preferred_element_type=jnp.float32)
        + jnp.dot(pooled, w_agg, preferred_element_type=jnp.float32)
    ).astype(jnp.bfloat16)
    result = jnp.dot(hidden, w_out, preferred_element_type=jnp.float32)
    center = jnp.mean(result, axis=-1, keepdims=True)
    spread = jnp.mean((result - center) ** 2, axis=-1, keepdims=True)
    normed = (result - center) * lax.rsqrt(spread + 1e-05) * norm_gain
    return (latent.astype(jnp.float32) + normed).astype(jnp.bfloat16)


def widen(field):
    collected = lax.all_gather(field, "gy", axis=1, tiled=True)
    collected = lax.all_gather(collected, "gz", axis=2, tiled=True)
    return extended(collected, (("gx", 0),), 1)


def shards(
    latents,
    offsets,
    neighbours,
    counts,
    w_recv,
    w_send,
    w_rel,
    b_first,
    w_edge,
    b_edge,
    w_self,
    w_agg,
    w_out,
    norm_gain,
):
    span_x, span_y, span_z = (latents.shape[0], latents.shape[1], latents.shape[2])
    latent_width = latents.shape[4]
    cell_count = span_x * span_y * span_z
    index_x = lax.axis_index("gx")
    index_y = lax.axis_index("gy")
    index_z = lax.axis_index("gz")
    whole_y = span_y * lax.axis_size("gy")
    whole_z = span_z * lax.axis_size("gz")
    base_x = index_x * span_x - 1
    ext_rows = (span_x + 2) * whole_y * whole_z * SLOTS
    cell_of = neighbours // SLOTS
    slot_of = neighbours % SLOTS
    coord_z = cell_of % whole_z
    coord_y = cell_of // whole_z % whole_y
    coord_x = cell_of // (whole_y * whole_z)
    local_ids = (
        (((coord_x - base_x) * whole_y + coord_y) * whole_z + coord_z) * SLOTS + slot_of
    ).reshape(cell_count, -1)
    sender_coords = (
        jnp.stack([coord_x, coord_y, coord_z], axis=-2)
        .astype(jnp.float32)
        .reshape(cell_count, 3, -1)
    )
    grid_x = (index_x * span_x + lax.iota(jnp.int32, span_x))[:, None, None]
    grid_y = (index_y * span_y + lax.iota(jnp.int32, span_y))[None, :, None]
    grid_z = (index_z * span_z + lax.iota(jnp.int32, span_z))[None, None, :]
    own_coords = jnp.stack([grid_x, grid_y, grid_z], axis=-1).astype(jnp.float32)
    own_places = (offsets.astype(jnp.float32) + own_coords[..., None]).reshape(cell_count, 3, SLOTS)
    rim_offsets = widen(offsets)
    offset_table = rim_offsets.transpose(3, 0, 1, 2, 4).reshape(3, ext_rows)
    count_rows = counts.reshape(cell_count)
    blocks_needed = (count_rows + SLOTS - 1) // SLOTS
    slot_ids = lax.iota(jnp.int32, SLOTS)
    current = latents.reshape(cell_count, SLOTS, latent_width)
    step_index = 0
    rimmed = widen(current.reshape(span_x, span_y, span_z, SLOTS, latent_width)).reshape(
        ext_rows, latent_width
    )
    rel_weight = w_rel[step_index].astype(jnp.float32)

    def senders(cell_index, block_index, rimmed=rimmed, step_index=step_index):
        sender_ids = lax.dynamic_slice_in_dim(local_ids[cell_index], block_index * SLOTS, SLOTS)
        gathered = jnp.take(rimmed, sender_ids, axis=0)
        send_term = jnp.dot(gathered, w_send[step_index], preferred_element_type=jnp.float32)
        send_place = jnp.take(offset_table, sender_ids, axis=1).astype(
            jnp.float32
        ) + lax.dynamic_slice_in_dim(sender_coords[cell_index], block_index * SLOTS, SLOTS, axis=1)
        live_mask = (block_index * SLOTS + slot_ids < count_rows[cell_index]).astype(jnp.float32)
        return (send_term, send_place, live_mask)

    def block_sum(
        cell_index,
        recv_term,
        first_block,
        last_block,
        step_index=step_index,
        rel_weight=rel_weight,
        senders=senders,
    ):

        def add_block(block_index, summed):
            send_term, send_place, live_mask = senders(cell_index, block_index)
            return summed + edge_sum(
                recv_term,
                send_term,
                own_places[cell_index],
                send_place,
                live_mask,
                rel_weight,
                w_edge[step_index],
                b_edge[step_index],
            )

        return lax.fori_loop(
            first_block, last_block, add_block, jnp.zeros((SLOTS, latent_width), jnp.float32)
        )

    recv_terms = (
        jnp.dot(
            current.reshape(-1, latent_width),
            w_recv[step_index],
            preferred_element_type=jnp.float32,
        )
        + b_first[step_index]
    ).reshape(cell_count, SLOTS, latent_width)
    sums = block_sum(0, recv_terms[0], 0, blocks_needed[0])
    current = jnp.stack(
        [
            renew(
                current[0],
                sums,
                w_self[step_index],
                w_agg[step_index],
                w_out[step_index],
                norm_gain[step_index],
            )
        ]
    )
    return current.reshape(span_x, span_y, span_z, SLOTS, latent_width)


def solution(mesh):
    in_specs = (
        P(("groups", "gx"), "gy", "gz", None, None),
        P(("groups", "gx"), "gy", "gz", None, None),
        P(("groups", "gx"), "gy", "gz", None),
        P(("groups", "gx"), "gy", "gz"),
        P(),
        P(),
        P(),
        P(),
        P(),
        P(),
        P(),
        P(),
        P(),
        P(),
    )
    out_specs = P(("groups", "gx"), "gy", "gz", None, None)
    return jax.shard_map(shards, mesh=mesh, in_specs=in_specs, out_specs=out_specs, check_vma=False)
```

profile of v0, /device:TPU:0, one launch (start us, length us, event | category | flops | bytes accessed | tf_op | source)
XLA Modules:
  0.0 117.4 jit_solution(15140709854701901017)
XLA Ops:
  0.0 5.9 %all_gather.14 = bf16[1,2,1,128,128]{4,3,2,0,1:T(8,128)(2,1)S(1)} all-gather(bf16[1,1,1,128,128]{4,3,2,0,1:T(8,128)(2,1)} %bitcast.142), channel_id=1, replica_groups=mesh['groups'=2,'gx'=4,'gy'=2,'gz'=2] {'gy'}, dimensions={1}, use_global_device_ids=true | all-gather | bytes 98304 | tf_op jit(solution)/shard_map/all_gather | solution.py:64
  5.9 2.0 %all_gather.15 = bf16[1,2,2,128,128]{4,3,2,1,0:T(8,128)(2,1)S(1)} all-gather(bf16[1,2,1,128,128]{4,3,2,1,0:T(8,128)(2,1)S(1)} %bitcast.144), channel_id=1, replica_groups=mesh['groups'=2,'gx'=4,'gy'=2,'gz'=2] {'gz'}, dimensions={2}, use_global_device_ids=true | all-gather | bytes 196608 | tf_op jit(solution)/shard_map/all_gather | solution.py:65
  7.9 4.1 %collective-permute-start.2 = (bf16[1,2,2,128,128]{4,3,2,1,0:T(8,128)(2,1)S(1)}, bf16[1,2,2,128,128]{4,3,2,1,0:T(8,128)(2,1)S(1)}, u32[]{:S(2)}, u32[]{:S(2)}) collective-permute-start(bf16[1,2,2,128,128]{4,3,2,1,0:T(8,128)(2,1)S(1)} %all_gather.15), channel_id=1, source_target_pairs={{0,4},{4,8},{8,12},{1,5},{5,9},{9,13},{2,6},{6,10},{10,14},{3,7},{... | collective-permute-start | bytes 393224 | tf_op jit(solution)/shard_map/ppermute | solution.py:16
  13.4 4.2 %all_gather.12 = bf16[1,2,1,3,128]{4,3,2,0,1:T(4,128)(2,1)S(1)} all-gather(bf16[1,1,1,3,128]{4,3,2,0,1:T(4,128)(2,1)S(1)} %bitcast.147), channel_id=1, replica_groups=mesh['groups'=2,'gx'=4,'gy'=2,'gz'=2] {'gy'}, dimensions={1}, use_global_device_ids=true | all-gather | bytes 2304 | tf_op jit(solution)/shard_map/all_gather | solution.py:64
  19.4 4.5 %collective-permute-start = (bf16[1,2,2,3,128]{4,3,2,0,1:T(4,128)(2,1)S(1)}, bf16[1,2,2,3,128]{4,3,2,0,1:T(4,128)(2,1)S(1)}, u32[]{:S(2)}, u32[]{:S(2)}) collective-permute-start(bf16[1,2,2,3,128]{4,3,2,0,1:T(4,128)(2,1)S(1)} %all_gather.13), channel_id=1, source_target_pairs={{0,4},{4,8},{8,12},{1,5},{5,9},{9,13},{2,6},{6,10},{10,14},{3,7},{... | collective-permute-start | bytes 9224 | tf_op jit(solution)/shard_map/ppermute | solution.py:16
  30.6 85.0 %while.23 = (s32[]{:T(128)}, f32[128,128]{1,0:T(8,128)S(1)}, s32[]{:T(128)}, f32[128,128]{1,0:T(8,128)S(1)}, f32[1,1,1,3,128]{4,3,2,1,0:T(4,128)S(1)}, /*index=5...) while((s32[]{:T(128)}, f32[128,128]{1,0:T(8,128)S(1)}, ...), condition=%wide.region_4.5_spmd.clone, body=%wide.region_0.4_spmd.clone.sunk | while | flops 90240648 | bytes 3800472 | solution.py:158
  33.3 25.6 %while.24 = (s32[]{:T(128)}, f32[8,16,128]{2,1,0:T(8,128)S(1)}, f32[8,16,128]{2,1,0:T(8,128)S(1)}, f32[128,128]{1,0:T(8,128)S(1)}, f32[3,128]{1,0:T(4,128)S(1)},...) while((s32[]{:T(128)}, f32[8,16,128]{2,1,0:T(8,128)S(1)}, ...), condition=%wide.region_3.3_spmd, body=%wide.region_1.2_spmd.sunk | while | flops 86009856 | bytes 3381177 | solution.py:47
  33.5 1.8 %multiply_convert_fusion.8 = bf16[16,128,128]{2,1,0:T(8,128)(2,1)S(1)} fusion(f32[128,128]{1,0:T(8,128)S(1)} %get-tuple-element.507, f32[16,128]{1,0:T(8,128)S(1)} %dynamic-slice_bitcast_fusion.2, f32[1,16,128]{2,0,1:T(1,128)S(1)} %bitcast.138, f32[3,16,128]{2,0,1:T(4,128)S(1)} %get-tuple-element.481, f32[4,128]{1,0:T(4,128)S(1)} %get-tuple-element.510), kind=kOutput, calls=%fused_computation.6.clone.1 | convolution fusion | flops 14426112 | bytes 632832 | tf_op jit(solution)/shard_map/while/body/while/body/eval_jaxpr/cij,cw->ijw/dot_general | solution.py:33
  36.7 1.8 %multiply_convert_fusion.8 = bf16[16,128,128]{2,1,0:T(8,128)(2,1)S(1)} fusion(f32[128,128]{1,0:T(8,128)S(1)} %get-tuple-element.507, f32[16,128]{1,0:T(8,128)S(1)} %dynamic-slice_bitcast_fusion.2, f32[1,16,128]{2,0,1:T(1,128)S(1)} %bitcast.138, f32[3,16,128]{2,0,1:T(4,128)S(1)} %get-tuple-element.481, f32[4,128]{1,0:T(4,128)S(1)} %get-tuple-element.510), kind=kOutput, calls=%fused_computation.6.clone.1 | convolution fusion | flops 14426112 | bytes 632832 | tf_op jit(solution)/shard_map/while/body/while/body/eval_jaxpr/cij,cw->ijw/dot_general | solution.py:33
  39.9 1.8 %multiply_convert_fusion.8 = bf16[16,128,128]{2,1,0:T(8,128)(2,1)S(1)} fusion(f32[128,128]{1,0:T(8,128)S(1)} %get-tuple-element.507, f32[16,128]{1,0:T(8,128)S(1)} %dynamic-slice_bitcast_fusion.2, f32[1,16,128]{2,0,1:T(1,128)S(1)} %bitcast.138, f32[3,16,128]{2,0,1:T(4,128)S(1)} %get-tuple-element.481, f32[4,128]{1,0:T(4,128)S(1)} %get-tuple-element.510), kind=kOutput, calls=%fused_computation.6.clone.1 | convolution fusion | flops 14426112 | bytes 632832 | tf_op jit(solution)/shard_map/while/body/while/body/eval_jaxpr/cij,cw->ijw/dot_general | solution.py:33
  43.1 1.8 %multiply_convert_fusion.8 = bf16[16,128,128]{2,1,0:T(8,128)(2,1)S(1)} fusion(f32[128,128]{1,0:T(8,128)S(1)} %get-tuple-element.507, f32[16,128]{1,0:T(8,128)S(1)} %dynamic-slice_bitcast_fusion.2, f32[1,16,128]{2,0,1:T(1,128)S(1)} %bitcast.138, f32[3,16,128]{2,0,1:T(4,128)S(1)} %get-tuple-element.481, f32[4,128]{1,0:T(4,128)S(1)} %get-tuple-element.510), kind=kOutput, calls=%fused_computation.6.clone.1 | convolution fusion | flops 14426112 | bytes 632832 | tf_op jit(solution)/shard_map/while/body/while/body/eval_jaxpr/cij,cw->ijw/dot_general | solution.py:33
  46.3 1.8 %multiply_convert_fusion.8 = bf16[16,128,128]{2,1,0:T(8,128)(2,1)S(1)} fusion(f32[128,128]{1,0:T(8,128)S(1)} %get-tuple-element.507, f32[16,128]{1,0:T(8,128)S(1)} %dynamic-slice_bitcast_fusion.2, f32[1,16,128]{2,0,1:T(1,128)S(1)} %bitcast.138, f32[3,16,128]{2,0,1:T(4,128)S(1)} %get-tuple-element.481, f32[4,128]{1,0:T(4,128)S(1)} %get-tuple-element.510), kind=kOutput, calls=%fused_computation.6.clone.1 | convolution fusion | flops 14426112 | bytes 632832 | tf_op jit(solution)/shard_map/while/body/while/body/eval_jaxpr/cij,cw->ijw/dot_general | solution.py:33
  49.5 1.8 %multiply_convert_fusion.8 = bf16[16,128,128]{2,1,0:T(8,128)(2,1)S(1)} fusion(f32[128,128]{1,0:T(8,128)S(1)} %get-tuple-element.507, f32[16,128]{1,0:T(8,128)S(1)} %dynamic-slice_bitcast_fusion.2, f32[1,16,128]{2,0,1:T(1,128)S(1)} %bitcast.138, f32[3,16,128]{2,0,1:T(4,128)S(1)} %get-tuple-element.481, f32[4,128]{1,0:T(4,128)S(1)} %get-tuple-element.510), kind=kOutput, calls=%fused_computation.6.clone.1 | convolution fusion | flops 14426112 | bytes 632832 | tf_op jit(solution)/shard_map/while/body/while/body/eval_jaxpr/cij,cw->ijw/dot_general | solution.py:33
  52.7 1.8 %multiply_convert_fusion.8 = bf16[16,128,128]{2,1,0:T(8,128)(2,1)S(1)} fusion(f32[128,128]{1,0:T(8,128)S(1)} %get-tuple-element.507, f32[16,128]{1,0:T(8,128)S(1)} %dynamic-slice_bitcast_fusion.2, f32[1,16,128]{2,0,1:T(1,128)S(1)} %bitcast.138, f32[3,16,128]{2,0,1:T(4,128)S(1)} %get-tuple-element.481, f32[4,128]{1,0:T(4,128)S(1)} %get-tuple-element.510), kind=kOutput, calls=%fused_computation.6.clone.1 | convolution fusion | flops 14426112 | bytes 632832 | tf_op jit(solution)/shard_map/while/body/while/body/eval_jaxpr/cij,cw->ijw/dot_general | solution.py:33
  55.9 1.8 %multiply_convert_fusion.8 = bf16[16,128,128]{2,1,0:T(8,128)(2,1)S(1)} fusion(f32[128,128]{1,0:T(8,128)S(1)} %get-tuple-element.507, f32[16,128]{1,0:T(8,128)S(1)} %dynamic-slice_bitcast_fusion.2, f32[1,16,128]{2,0,1:T(1,128)S(1)} %bitcast.138, f32[3,16,128]{2,0,1:T(4,128)S(1)} %get-tuple-element.481, f32[4,128]{1,0:T(4,128)S(1)} %get-tuple-element.510), kind=kOutput, calls=%fused_computation.6.clone.1 | convolution fusion | flops 14426112 | bytes 632832 | tf_op jit(solution)/shard_map/while/body/while/body/eval_jaxpr/cij,cw->ijw/dot_general | solution.py:33
  61.6 25.6 %while.24 = (s32[]{:T(128)}, f32[8,16,128]{2,1,0:T(8,128)S(1)}, f32[8,16,128]{2,1,0:T(8,128)S(1)}, f32[128,128]{1,0:T(8,128)S(1)}, f32[3,128]{1,0:T(4,128)S(1)},...) while((s32[]{:T(128)}, f32[8,16,128]{2,1,0:T(8,128)S(1)}, ...), condition=%wide.region_3.3_spmd, body=%wide.region_1.2_spmd.sunk | while | flops 86009856 | bytes 3381177 | solution.py:47
  61.8 1.8 %multiply_convert_fusion.8 = bf16[16,128,128]{2,1,0:T(8,128)(2,1)S(1)} fusion(f32[128,128]{1,0:T(8,128)S(1)} %get-tuple-element.507, f32[16,128]{1,0:T(8,128)S(1)} %dynamic-slice_bitcast_fusion.2, f32[1,16,128]{2,0,1:T(1,128)S(1)} %bitcast.138, f32[3,16,128]{2,0,1:T(4,128)S(1)} %get-tuple-element.481, f32[4,128]{1,0:T(4,128)S(1)} %get-tuple-element.510), kind=kOutput, calls=%fused_computation.6.clone.1 | convolution fusion | flops 14426112 | bytes 632832 | tf_op jit(solution)/shard_map/while/body/while/body/eval_jaxpr/cij,cw->ijw/dot_general | solution.py:33
  65.0 1.8 %multiply_convert_fusion.8 = bf16[16,128,128]{2,1,0:T(8,128)(2,1)S(1)} fusion(f32[128,128]{1,0:T(8,128)S(1)} %get-tuple-element.507, f32[16,128]{1,0:T(8,128)S(1)} %dynamic-slice_bitcast_fusion.2, f32[1,16,128]{2,0,1:T(1,128)S(1)} %bitcast.138, f32[3,16,128]{2,0,1:T(4,128)S(1)} %get-tuple-element.481, f32[4,128]{1,0:T(4,128)S(1)} %get-tuple-element.510), kind=kOutput, calls=%fused_computation.6.clone.1 | convolution fusion | flops 14426112 | bytes 632832 | tf_op jit(solution)/shard_map/while/body/while/body/eval_jaxpr/cij,cw->ijw/dot_general | solution.py:33
  68.2 1.8 %multiply_convert_fusion.8 = bf16[16,128,128]{2,1,0:T(8,128)(2,1)S(1)} fusion(f32[128,128]{1,0:T(8,128)S(1)} %get-tuple-element.507, f32[16,128]{1,0:T(8,128)S(1)} %dynamic-slice_bitcast_fusion.2, f32[1,16,128]{2,0,1:T(1,128)S(1)} %bitcast.138, f32[3,16,128]{2,0,1:T(4,128)S(1)} %get-tuple-element.481, f32[4,128]{1,0:T(4,128)S(1)} %get-tuple-element.510), kind=kOutput, calls=%fused_computation.6.clone.1 | convolution fusion | flops 14426112 | bytes 632832 | tf_op jit(solution)/shard_map/while/body/while/body/eval_jaxpr/cij,cw->ijw/dot_general | solution.py:33
  71.4 1.8 %multiply_convert_fusion.8 = bf16[16,128,128]{2,1,0:T(8,128)(2,1)S(1)} fusion(f32[128,128]{1,0:T(8,128)S(1)} %get-tuple-element.507, f32[16,128]{1,0:T(8,128)S(1)} %dynamic-slice_bitcast_fusion.2, f32[1,16,128]{2,0,1:T(1,128)S(1)} %bitcast.138, f32[3,16,128]{2,0,1:T(4,128)S(1)} %get-tuple-element.481, f32[4,128]{1,0:T(4,128)S(1)} %get-tuple-element.510), kind=kOutput, calls=%fused_computation.6.clone.1 | convolution fusion | flops 14426112 | bytes 632832 | tf_op jit(solution)/shard_map/while/body/while/body/eval_jaxpr/cij,cw->ijw/dot_general | solution.py:33
  74.6 1.8 %multiply_convert_fusion.8 = bf16[16,128,128]{2,1,0:T(8,128)(2,1)S(1)} fusion(f32[128,128]{1,0:T(8,128)S(1)} %get-tuple-element.507, f32[16,128]{1,0:T(8,128)S(1)} %dynamic-slice_bitcast_fusion.2, f32[1,16,128]{2,0,1:T(1,128)S(1)} %bitcast.138, f32[3,16,128]{2,0,1:T(4,128)S(1)} %get-tuple-element.481, f32[4,128]{1,0:T(4,128)S(1)} %get-tuple-element.510), kind=kOutput, calls=%fused_computation.6.clone.1 | convolution fusion | flops 14426112 | bytes 632832 | tf_op jit(solution)/shard_map/while/body/while/body/eval_jaxpr/cij,cw->ijw/dot_general | solution.py:33
  77.8 1.8 %multiply_convert_fusion.8 = bf16[16,128,128]{2,1,0:T(8,128)(2,1)S(1)} fusion(f32[128,128]{1,0:T(8,128)S(1)} %get-tuple-element.507, f32[16,128]{1,0:T(8,128)S(1)} %dynamic-slice_bitcast_fusion.2, f32[1,16,128]{2,0,1:T(1,128)S(1)} %bitcast.138, f32[3,16,128]{2,0,1:T(4,128)S(1)} %get-tuple-element.481, f32[4,128]{1,0:T(4,128)S(1)} %get-tuple-element.510), kind=kOutput, calls=%fused_computation.6.clone.1 | convolution fusion | flops 14426112 | bytes 632832 | tf_op jit(solution)/shard_map/while/body/while/body/eval_jaxpr/cij,cw->ijw/dot_general | solution.py:33
  81.0 1.8 %multiply_convert_fusion.8 = bf16[16,128,128]{2,1,0:T(8,128)(2,1)S(1)} fusion(f32[128,128]{1,0:T(8,128)S(1)} %get-tuple-element.507, f32[16,128]{1,0:T(8,128)S(1)} %dynamic-slice_bitcast_fusion.2, f32[1,16,128]{2,0,1:T(1,128)S(1)} %bitcast.138, f32[3,16,128]{2,0,1:T(4,128)S(1)} %get-tuple-element.481, f32[4,128]{1,0:T(4,128)S(1)} %get-tuple-element.510), kind=kOutput, calls=%fused_computation.6.clone.1 | convolution fusion | flops 14426112 | bytes 632832 | tf_op jit(solution)/shard_map/while/body/while/body/eval_jaxpr/cij,cw->ijw/dot_general | solution.py:33
  84.2 1.8 %multiply_convert_fusion.8 = bf16[16,128,128]{2,1,0:T(8,128)(2,1)S(1)} fusion(f32[128,128]{1,0:T(8,128)S(1)} %get-tuple-element.507, f32[16,128]{1,0:T(8,128)S(1)} %dynamic-slice_bitcast_fusion.2, f32[1,16,128]{2,0,1:T(1,128)S(1)} %bitcast.138, f32[3,16,128]{2,0,1:T(4,128)S(1)} %get-tuple-element.481, f32[4,128]{1,0:T(4,128)S(1)} %get-tuple-element.510), kind=kOutput, calls=%fused_computation.6.clone.1 | convolution fusion | flops 14426112 | bytes 632832 | tf_op jit(solution)/shard_map/while/body/while/body/eval_jaxpr/cij,cw->ijw/dot_general | solution.py:33
  89.9 25.6 %while.24 = (s32[]{:T(128)}, f32[8,16,128]{2,1,0:T(8,128)S(1)}, f32[8,16,128]{2,1,0:T(8,128)S(1)}, f32[128,128]{1,0:T(8,128)S(1)}, f32[3,128]{1,0:T(4,128)S(1)},...) while((s32[]{:T(128)}, f32[8,16,128]{2,1,0:T(8,128)S(1)}, ...), condition=%wide.region_3.3_spmd, body=%wide.region_1.2_spmd.sunk | while | flops 86009856 | bytes 3381177 | solution.py:47
  90.2 1.8 %multiply_convert_fusion.8 = bf16[16,128,128]{2,1,0:T(8,128)(2,1)S(1)} fusion(f32[128,128]{1,0:T(8,128)S(1)} %get-tuple-element.507, f32[16,128]{1,0:T(8,128)S(1)} %dynamic-slice_bitcast_fusion.2, f32[1,16,128]{2,0,1:T(1,128)S(1)} %bitcast.138, f32[3,16,128]{2,0,1:T(4,128)S(1)} %get-tuple-element.481, f32[4,128]{1,0:T(4,128)S(1)} %get-tuple-element.510), kind=kOutput, calls=%fused_computation.6.clone.1 | convolution fusion | flops 14426112 | bytes 632832 | tf_op jit(solution)/shard_map/while/body/while/body/eval_jaxpr/cij,cw->ijw/dot_general | solution.py:33
  93.4 1.8 %multiply_convert_fusion.8 = bf16[16,128,128]{2,1,0:T(8,128)(2,1)S(1)} fusion(f32[128,128]{1,0:T(8,128)S(1)} %get-tuple-element.507, f32[16,128]{1,0:T(8,128)S(1)} %dynamic-slice_bitcast_fusion.2, f32[1,16,128]{2,0,1:T(1,128)S(1)} %bitcast.138, f32[3,16,128]{2,0,1:T(4,128)S(1)} %get-tuple-element.481, f32[4,128]{1,0:T(4,128)S(1)} %get-tuple-element.510), kind=kOutput, calls=%fused_computation.6.clone.1 | convolution fusion | flops 14426112 | bytes 632832 | tf_op jit(solution)/shard_map/while/body/while/body/eval_jaxpr/cij,cw->ijw/dot_general | solution.py:33
  96.6 1.8 %multiply_convert_fusion.8 = bf16[16,128,128]{2,1,0:T(8,128)(2,1)S(1)} fusion(f32[128,128]{1,0:T(8,128)S(1)} %get-tuple-element.507, f32[16,128]{1,0:T(8,128)S(1)} %dynamic-slice_bitcast_fusion.2, f32[1,16,128]{2,0,1:T(1,128)S(1)} %bitcast.138, f32[3,16,128]{2,0,1:T(4,128)S(1)} %get-tuple-element.481, f32[4,128]{1,0:T(4,128)S(1)} %get-tuple-element.510), kind=kOutput, calls=%fused_computation.6.clone.1 | convolution fusion | flops 14426112 | bytes 632832 | tf_op jit(solution)/shard_map/while/body/while/body/eval_jaxpr/cij,cw->ijw/dot_general | solution.py:33
  99.8 1.8 %multiply_convert_fusion.8 = bf16[16,128,128]{2,1,0:T(8,128)(2,1)S(1)} fusion(f32[128,128]{1,0:T(8,128)S(1)} %get-tuple-element.507, f32[16,128]{1,0:T(8,128)S(1)} %dynamic-slice_bitcast_fusion.2, f32[1,16,128]{2,0,1:T(1,128)S(1)} %bitcast.138, f32[3,16,128]{2,0,1:T(4,128)S(1)} %get-tuple-element.481, f32[4,128]{1,0:T(4,128)S(1)} %get-tuple-element.510), kind=kOutput, calls=%fused_computation.6.clone.1 | convolution fusion | flops 14426112 | bytes 632832 | tf_op jit(solution)/shard_map/while/body/while/body/eval_jaxpr/cij,cw->ijw/dot_general | solution.py:33
  103.0 1.8 %multiply_convert_fusion.8 = bf16[16,128,128]{2,1,0:T(8,128)(2,1)S(1)} fusion(f32[128,128]{1,0:T(8,128)S(1)} %get-tuple-element.507, f32[16,128]{1,0:T(8,128)S(1)} %dynamic-slice_bitcast_fusion.2, f32[1,16,128]{2,0,1:T(1,128)S(1)} %bitcast.138, f32[3,16,128]{2,0,1:T(4,128)S(1)} %get-tuple-element.481, f32[4,128]{1,0:T(4,128)S(1)} %get-tuple-element.510), kind=kOutput, calls=%fused_computation.6.clone.1 | convolution fusion | flops 14426112 | bytes 632832 | tf_op jit(solution)/shard_map/while/body/while/body/eval_jaxpr/cij,cw->ijw/dot_general | solution.py:33
  106.2 1.8 %multiply_convert_fusion.8 = bf16[16,128,128]{2,1,0:T(8,128)(2,1)S(1)} fusion(f32[128,128]{1,0:T(8,128)S(1)} %get-tuple-element.507, f32[16,128]{1,0:T(8,128)S(1)} %dynamic-slice_bitcast_fusion.2, f32[1,16,128]{2,0,1:T(1,128)S(1)} %bitcast.138, f32[3,16,128]{2,0,1:T(4,128)S(1)} %get-tuple-element.481, f32[4,128]{1,0:T(4,128)S(1)} %get-tuple-element.510), kind=kOutput, calls=%fused_computation.6.clone.1 | convolution fusion | flops 14426112 | bytes 632832 | tf_op jit(solution)/shard_map/while/body/while/body/eval_jaxpr/cij,cw->ijw/dot_general | solution.py:33
  109.4 1.8 %multiply_convert_fusion.8 = bf16[16,128,128]{2,1,0:T(8,128)(2,1)S(1)} fusion(f32[128,128]{1,0:T(8,128)S(1)} %get-tuple-element.507, f32[16,128]{1,0:T(8,128)S(1)} %dynamic-slice_bitcast_fusion.2, f32[1,16,128]{2,0,1:T(1,128)S(1)} %bitcast.138, f32[3,16,128]{2,0,1:T(4,128)S(1)} %get-tuple-element.481, f32[4,128]{1,0:T(4,128)S(1)} %get-tuple-element.510), kind=kOutput, calls=%fused_computation.6.clone.1 | convolution fusion | flops 14426112 | bytes 632832 | tf_op jit(solution)/shard_map/while/body/while/body/eval_jaxpr/cij,cw->ijw/dot_general | solution.py:33
  (311 shorter events, 51.6 us)
Async XLA Ops:
  0.0 115.6 %copy-start = (bf16[1,128,128]{2,1,0:T(8,128)(2,1)S(1)}, bf16[1,128,128]{2,1,0:T(8,128)(2,1)}, u32[]{:S(2)}) copy-start(bf16[1,128,128]{2,1,0:T(8,128)(2,1)} %param.30) | copy-start | bytes 98308
  5.9 7.4 %copy-start.6 = (bf16[1,1,1,3,128]{4,3,2,1,0:T(4,128)(2,1)S(1)}, bf16[1,1,1,3,128]{4,3,2,1,0:T(4,128)(2,1)}, u32[]{:S(2)}) copy-start(bf16[1,1,1,3,128]{4,3,2,1,0:T(4,128)(2,1)} %param.19) | copy-start | bytes 2308
  5.9 19.3 %copy-start.5 = (s32[1,1,1,384]{3,2,1,0:T(1,128)S(1)}, s32[1,1,1,384]{3,2,1,0:T(1,128)}, u32[]{:S(2)}) copy-start(s32[1,1,1,384]{3,2,1,0:T(1,128)} %param.20) | copy-start | bytes 4612
  5.9 20.1 %copy-start.3 = (bf16[1,128,128]{2,1,0:T(8,128)(2,1)S(1)}, bf16[1,128,128]{2,1,0:T(8,128)(2,1)}, u32[]{:S(2)}) copy-start(bf16[1,128,128]{2,1,0:T(8,128)(2,1)} %param.28) | copy-start | bytes 98308
  7.9 18.1 %copy-start.2 = (bf16[1,1,1,128,128]{4,3,2,1,0:T(8,128)(2,1)S(1)}, bf16[1,1,1,128,128]{4,3,2,1,0:T(8,128)(2,1)}, u32[]{:S(2)}) copy-start(bf16[1,1,1,128,128]{4,3,2,1,0:T(8,128)(2,1)} %param.18) | copy-start | bytes 98308
  7.9 21.8 %collective-permute-start.2 = (bf16[1,2,2,128,128]{4,3,2,1,0:T(8,128)(2,1)S(1)}, bf16[1,2,2,128,128]{4,3,2,1,0:T(8,128)(2,1)S(1)}, u32[]{:S(2)}, u32[]{:S(2)}) collective-permute-start(bf16[1,2,2,128,128]{4,3,2,1,0:T(8,128)(2,1)S(1)} %all_gather.15), channel_id=1, source_target_pairs={{0,4},{4,8},{8,12},{1,5},{5,9},{9,13},{2,6},{6,10},{10,14},{3,7},{... | collective-permute-start | bytes 393224 | tf_op jit(solution)/shard_map/ppermute | solution.py:16
  12.0 17.7 %collective-permute-start.3 = (bf16[1,2,2,128,128]{4,3,2,1,0:T(8,128)(2,1)S(1)}, bf16[1,2,2,128,128]{4,3,2,1,0:T(8,128)(2,1)S(1)}, u32[]{:S(2)}, u32[]{:S(2)}) collective-permute-start(bf16[1,2,2,128,128]{4,3,2,1,0:T(8,128)(2,1)S(1)} %all_gather.15), channel_id=1, source_target_pairs={{4,0},{8,4},{12,8},{5,1},{9,5},{13,9},{6,2},{10,6},{14,10},{7,3},{... | collective-permute-start | bytes 393224 | tf_op jit(solution)/shard_map/ppermute | solution.py:17
  19.4 8.5 %collective-permute-start = (bf16[1,2,2,3,128]{4,3,2,0,1:T(4,128)(2,1)S(1)}, bf16[1,2,2,3,128]{4,3,2,0,1:T(4,128)(2,1)S(1)}, u32[]{:S(2)}, u32[]{:S(2)}) collective-permute-start(bf16[1,2,2,3,128]{4,3,2,0,1:T(4,128)(2,1)S(1)} %all_gather.13), channel_id=1, source_target_pairs={{0,4},{4,8},{8,12},{1,5},{5,9},{9,13},{2,6},{6,10},{10,14},{3,7},{... | collective-permute-start | bytes 9224 | tf_op jit(solution)/shard_map/ppermute | solution.py:16
  23.9 5.5 %collective-permute-start.1 = (bf16[1,2,2,3,128]{4,3,2,0,1:T(4,128)(2,1)S(1)}, bf16[1,2,2,3,128]{4,3,2,0,1:T(4,128)(2,1)S(1)}, u32[]{:S(2)}, u32[]{:S(2)}) collective-permute-start(bf16[1,2,2,3,128]{4,3,2,0,1:T(4,128)(2,1)S(1)} %all_gather.13), channel_id=1, source_target_pairs={{4,0},{8,4},{12,8},{5,1},{9,5},{13,9},{6,2},{10,6},{14,10},{7,3},{... | collective-permute-start | bytes 9224 | tf_op jit(solution)/shard_map/ppermute | solution.py:17
  25.4 0.7 copy-start.7
  26.1 0.8 copy-start.4
  26.2 0.7 copy-start.8
  29.8 0.8 copy-start.1
  29.8 0.8 copy-start.10
  29.8 0.8 copy-start.12
  30.6 85.0 %copy-start.11 = (bf16[1,128,128]{2,1,0:T(8,128)(2,1)S(1)}, bf16[1,128,128]{2,1,0:T(8,128)(2,1)}, u32[]{:S(2)}) copy-start(bf16[1,128,128]{2,1,0:T(8,128)(2,1)} %param.29) | copy-start | bytes 98308
  116.0 0.7 copy-start.9
where the time goes:
time: 118 us; the launch traced here: 117 us
  matrix products  71.3 us (60%)
  blocking collectives  14 us (12%)
  local copies, waits for them, and re-layouts  11.5 us (10%)
  starting transfers between devices  11.2 us (9%)
  other arithmetic  5.12 us (4%)
  loops' own time  1.81 us (2%)
  waiting for transfers between devices  1.59 us (1%)
    dot_general x24, matrix products, tile_messages(): jnp.einsum('cij,cw->ijw', features, rel_weight, precision=lax.Precision.H...  44.2 us
    dot_general x24, matrix products, tile_messages(): jnp.einsum('ijw,j->iw', message, live_mask, precision=lax.Precision.HIGHEST)  15.6 us
    dot_general x24, matrix products, tile_messages(): jnp.dot(edge_act.reshape(-1, latent_width), w_edge, preferred_element_typ...  10.3 us
    all_gather x2, blocking collectives, widen(): collected = lax.all_gather(field, 'gy', axis=1, tiled=True)  10.2 us
    ppermute x2, starting transfers between devices, extended(): before = lax.ppermute(last, axis, up)  8.62 us
    all_gather x2, blocking collectives, widen(): collected = lax.all_gather(collected, 'gz', axis=2, tiled=True)  3.82 us
    unnamed x28, local copies, waits for them, and re-layouts  3.08 us
    ppermute x2, starting transfers between devices, extended(): after = lax.ppermute(first, axis, down)  2.58 us
  transfers between devices with their start and end apart: 4, of which 1 were waited for; matrix products, arithmetic and copies ran while one was open for 1% of the time, Pallas kernels for 0%

commit v1 on v0

--- a/solution.py
+++ b/solution.py
@@ -61,7 +61,7 @@
 
 
 def widen(field):
-    collected = lax.all_gather(field, "gy", axis=1, tiled=True)
+    collected = jnp.concatenate(lax.all_gather(field, axis_name="gy"), 1)
     collected = lax.all_gather(collected, "gz", axis=2, tiled=True)
     return extended(collected, (("gx", 0),), 1)
 

time: 118 us -> 118 us (level)
  no operation moved by 1% of the time
where the time goes in v1:
time: 118 us; the launch traced here: 117 us
  matrix products  71.3 us (60%)
  blocking collectives  14 us (12%)
  local copies, waits for them, and re-layouts  11.5 us (10%)
  starting transfers between devices  11.2 us (9%)
  other arithmetic  5.11 us (4%)
  loops' own time  1.81 us (2%)
  waiting for transfers between devices  1.59 us (1%)
    dot_general x24, matrix products, tile_messages(): jnp.einsum('cij,cw->ijw', features, rel_weight, precision=lax.Precision.H...  44.2 us
    dot_general x24, matrix products, tile_messages(): jnp.einsum('ijw,j->iw', message, live_mask, precision=lax.Precision.HIGHEST)  15.6 us
    dot_general x24, matrix products, tile_messages(): jnp.dot(edge_act.reshape(-1, latent_width), w_edge, preferred_element_typ...  10.3 us
    all_gather x2, blocking collectives, widen(): collected = jnp.concatenate(lax.all_gather(field, axis_name='gy'), 1)  10.2 us
    ppermute x2, starting transfers between devices, extended(): before = lax.ppermute(last, axis, up)  8.62 us
    all_gather x2, blocking collectives, widen(): collected = lax.all_gather(collected, 'gz', axis=2, tiled=True)  3.82 us
    unnamed x28, local copies, waits for them, and re-layouts  3.07 us
    ppermute x2, starting transfers between devices, extended(): after = lax.ppermute(first, axis, down)  2.58 us
  transfers between devices with their start and end apart: 4, of which 1 were waited for; matrix products, arithmetic and copies ran while one was open for 1% of the time, Pallas kernels for 0%

profile of v1, /device:TPU:0, one launch (start us, length us, event | category | flops | bytes accessed | tf_op | source)
XLA Modules:
  0.0 117.5 jit_solution(3612230980208086968)
XLA Ops:
  0.0 5.9 %all-gather.2 = bf16[2,1,1,128,128]{4,3,2,1,0:T(8,128)(2,1)S(1)} all-gather(bf16[1,1,1,128,128]{4,3,2,1,0:T(8,128)(2,1)} %param.18), channel_id=4, replica_groups=mesh['groups'=2,'gx'=4,'gy'=2,'gz'=2] {'gy'}, dimensions={0}, use_global_device_ids=true | all-gather | bytes 98304 | tf_op jit(solution)/shard_map/all_gather | solution.py:64
  5.9 2.0 %all-gather.3 = bf16[2,2,1,128,128]{4,3,2,1,0:T(8,128)(2,1)S(1)} all-gather(bf16[2,1,1,128,128]{4,3,2,1,0:T(8,128)(2,1)S(1)} %all-gather.2), channel_id=5, replica_groups=mesh['groups'=2,'gx'=4,'gy'=2,'gz'=2] {'gz'}, dimensions={1}, use_global_device_ids=true | all-gather | bytes 196608 | tf_op jit(solution)/shard_map/all_gather | solution.py:65
  7.9 4.1 %collective-permute-start.2 = (bf16[1,2,2,128,128]{4,3,2,1,0:T(8,128)(2,1)S(1)}, bf16[1,2,2,128,128]{4,3,2,1,0:T(8,128)(2,1)S(1)}, u32[]{:S(2)}, u32[]{:S(2)}) collective-permute-start(bf16[1,2,2,128,128]{4,3,2,1,0:T(8,128)(2,1)S(1)} %bitcast.141), channel_id=1, source_target_pairs={{0,4},{4,8},{8,12},{1,5},{5,9},{9,13},{2,6},{6,10},{10,14},{3,7},{... | collective-permute-start | bytes 393224 | tf_op jit(solution)/shard_map/ppermute | solution.py:16
  13.4 4.2 %all-gather = bf16[2,1,1,3,128]{4,3,2,1,0:T(4,128)(2,1)S(1)} all-gather(bf16[1,1,1,3,128]{4,3,2,1,0:T(4,128)(2,1)S(1)} %copy-done.6), channel_id=2, replica_groups=mesh['groups'=2,'gx'=4,'gy'=2,'gz'=2] {'gy'}, dimensions={0}, use_global_device_ids=true | all-gather | bytes 2304 | tf_op jit(solution)/shard_map/all_gather | solution.py:64
  19.4 4.5 %collective-permute-start = (bf16[1,2,2,3,128]{4,3,2,1,0:T(4,128)(2,1)S(1)}, bf16[1,2,2,3,128]{4,3,2,1,0:T(4,128)(2,1)S(1)}, u32[]{:S(2)}, u32[]{:S(2)}) collective-permute-start(bf16[1,2,2,3,128]{4,3,2,1,0:T(4,128)(2,1)S(1)} %bitcast.145), channel_id=1, source_target_pairs={{0,4},{4,8},{8,12},{1,5},{5,9},{9,13},{2,6},{6,10},{10,14},{3,7},{... | collective-permute-start | bytes 9224 | tf_op jit(solution)/shard_map/ppermute | solution.py:16
  30.6 85.0 %while.23 = (s32[]{:T(128)}, f32[128,128]{1,0:T(8,128)S(1)}, s32[]{:T(128)}, f32[128,128]{1,0:T(8,128)S(1)}, f32[1,1,1,3,128]{4,3,2,1,0:T(4,128)S(1)}, /*index=5...) while((s32[]{:T(128)}, f32[128,128]{1,0:T(8,128)S(1)}, ...), condition=%wide.region_4.5_spmd.clone, body=%wide.region_0.4_spmd.clone.sunk | while | flops 90240648 | bytes 3800472 | solution.py:158
  33.3 25.6 %while.24 = (s32[]{:T(128)}, f32[8,16,128]{2,1,0:T(8,128)S(1)}, f32[8,16,128]{2,1,0:T(8,128)S(1)}, f32[128,128]{1,0:T(8,128)S(1)}, f32[3,128]{1,0:T(4,128)S(1)},...) while((s32[]{:T(128)}, f32[8,16,128]{2,1,0:T(8,128)S(1)}, ...), condition=%wide.region_3.3_spmd, body=%wide.region_1.2_spmd.sunk | while | flops 86009856 | bytes 3381177 | solution.py:47
  33.5 1.8 %multiply_convert_fusion.8 = bf16[16,128,128]{2,1,0:T(8,128)(2,1)S(1)} fusion(f32[128,128]{1,0:T(8,128)S(1)} %get-tuple-element.507, f32[16,128]{1,0:T(8,128)S(1)} %dynamic-slice_bitcast_fusion.2, f32[1,16,128]{2,0,1:T(1,128)S(1)} %bitcast.137, f32[3,16,128]{2,0,1:T(4,128)S(1)} %get-tuple-element.481, f32[4,128]{1,0:T(4,128)S(1)} %get-tuple-element.510), kind=kOutput, calls=%fused_computation.6.clone.1 | convolution fusion | flops 14426112 | bytes 632832 | tf_op jit(solution)/shard_map/while/body/while/body/eval_jaxpr/cij,cw->ijw/dot_general | solution.py:33
  36.7 1.8 %multiply_convert_fusion.8 = bf16[16,128,128]{2,1,0:T(8,128)(2,1)S(1)} fusion(f32[128,128]{1,0:T(8,128)S(1)} %get-tuple-element.507, f32[16,128]{1,0:T(8,128)S(1)} %dynamic-slice_bitcast_fusion.2, f32[1,16,128]{2,0,1:T(1,128)S(1)} %bitcast.137, f32[3,16,128]{2,0,1:T(4,128)S(1)} %get-tuple-element.481, f32[4,128]{1,0:T(4,128)S(1)} %get-tuple-element.510), kind=kOutput, calls=%fused_computation.6.clone.1 | convolution fusion | flops 14426112 | bytes 632832 | tf_op jit(solution)/shard_map/while/body/while/body/eval_jaxpr/cij,cw->ijw/dot_general | solution.py:33
  39.9 1.8 %multiply_convert_fusion.8 = bf16[16,128,128]{2,1,0:T(8,128)(2,1)S(1)} fusion(f32[128,128]{1,0:T(8,128)S(1)} %get-tuple-element.507, f32[16,128]{1,0:T(8,128)S(1)} %dynamic-slice_bitcast_fusion.2, f32[1,16,128]{2,0,1:T(1,128)S(1)} %bitcast.137, f32[3,16,128]{2,0,1:T(4,128)S(1)} %get-tuple-element.481, f32[4,128]{1,0:T(4,128)S(1)} %get-tuple-element.510), kind=kOutput, calls=%fused_computation.6.clone.1 | convolution fusion | flops 14426112 | bytes 632832 | tf_op jit(solution)/shard_map/while/body/while/body/eval_jaxpr/cij,cw->ijw/dot_general | solution.py:33
  43.1 1.8 %multiply_convert_fusion.8 = bf16[16,128,128]{2,1,0:T(8,128)(2,1)S(1)} fusion(f32[128,128]{1,0:T(8,128)S(1)} %get-tuple-element.507, f32[16,128]{1,0:T(8,128)S(1)} %dynamic-slice_bitcast_fusion.2, f32[1,16,128]{2,0,1:T(1,128)S(1)} %bitcast.137, f32[3,16,128]{2,0,1:T(4,128)S(1)} %get-tuple-element.481, f32[4,128]{1,0:T(4,128)S(1)} %get-tuple-element.510), kind=kOutput, calls=%fused_computation.6.clone.1 | convolution fusion | flops 14426112 | bytes 632832 | tf_op jit(solution)/shard_map/while/body/while/body/eval_jaxpr/cij,cw->ijw/dot_general | solution.py:33
  46.3 1.8 %multiply_convert_fusion.8 = bf16[16,128,128]{2,1,0:T(8,128)(2,1)S(1)} fusion(f32[128,128]{1,0:T(8,128)S(1)} %get-tuple-element.507, f32[16,128]{1,0:T(8,128)S(1)} %dynamic-slice_bitcast_fusion.2, f32[1,16,128]{2,0,1:T(1,128)S(1)} %bitcast.137, f32[3,16,128]{2,0,1:T(4,128)S(1)} %get-tuple-element.481, f32[4,128]{1,0:T(4,128)S(1)} %get-tuple-element.510), kind=kOutput, calls=%fused_computation.6.clone.1 | convolution fusion | flops 14426112 | bytes 632832 | tf_op jit(solution)/shard_map/while/body/while/body/eval_jaxpr/cij,cw->ijw/dot_general | solution.py:33
  49.5 1.8 %multiply_convert_fusion.8 = bf16[16,128,128]{2,1,0:T(8,128)(2,1)S(1)} fusion(f32[128,128]{1,0:T(8,128)S(1)} %get-tuple-element.507, f32[16,128]{1,0:T(8,128)S(1)} %dynamic-slice_bitcast_fusion.2, f32[1,16,128]{2,0,1:T(1,128)S(1)} %bitcast.137, f32[3,16,128]{2,0,1:T(4,128)S(1)} %get-tuple-element.481, f32[4,128]{1,0:T(4,128)S(1)} %get-tuple-element.510), kind=kOutput, calls=%fused_computation.6.clone.1 | convolution fusion | flops 14426112 | bytes 632832 | tf_op jit(solution)/shard_map/while/body/while/body/eval_jaxpr/cij,cw->ijw/dot_general | solution.py:33
  52.7 1.8 %multiply_convert_fusion.8 = bf16[16,128,128]{2,1,0:T(8,128)(2,1)S(1)} fusion(f32[128,128]{1,0:T(8,128)S(1)} %get-tuple-element.507, f32[16,128]{1,0:T(8,128)S(1)} %dynamic-slice_bitcast_fusion.2, f32[1,16,128]{2,0,1:T(1,128)S(1)} %bitcast.137, f32[3,16,128]{2,0,1:T(4,128)S(1)} %get-tuple-element.481, f32[4,128]{1,0:T(4,128)S(1)} %get-tuple-element.510), kind=kOutput, calls=%fused_computation.6.clone.1 | convolution fusion | flops 14426112 | bytes 632832 | tf_op jit(solution)/shard_map/while/body/while/body/eval_jaxpr/cij,cw->ijw/dot_general | solution.py:33
  55.9 1.8 %multiply_convert_fusion.8 = bf16[16,128,128]{2,1,0:T(8,128)(2,1)S(1)} fusion(f32[128,128]{1,0:T(8,128)S(1)} %get-tuple-element.507, f32[16,128]{1,0:T(8,128)S(1)} %dynamic-slice_bitcast_fusion.2, f32[1,16,128]{2,0,1:T(1,128)S(1)} %bitcast.137, f32[3,16,128]{2,0,1:T(4,128)S(1)} %get-tuple-element.481, f32[4,128]{1,0:T(4,128)S(1)} %get-tuple-element.510), kind=kOutput, calls=%fused_computation.6.clone.1 | convolution fusion | flops 14426112 | bytes 632832 | tf_op jit(solution)/shard_map/while/body/while/body/eval_jaxpr/cij,cw->ijw/dot_general | solution.py:33
  61.6 25.6 %while.24 = (s32[]{:T(128)}, f32[8,16,128]{2,1,0:T(8,128)S(1)}, f32[8,16,128]{2,1,0:T(8,128)S(1)}, f32[128,128]{1,0:T(8,128)S(1)}, f32[3,128]{1,0:T(4,128)S(1)},...) while((s32[]{:T(128)}, f32[8,16,128]{2,1,0:T(8,128)S(1)}, ...), condition=%wide.region_3.3_spmd, body=%wide.region_1.2_spmd.sunk | while | flops 86009856 | bytes 3381177 | solution.py:47
  61.9 1.8 %multiply_convert_fusion.8 = bf16[16,128,128]{2,1,0:T(8,128)(2,1)S(1)} fusion(f32[128,128]{1,0:T(8,128)S(1)} %get-tuple-element.507, f32[16,128]{1,0:T(8,128)S(1)} %dynamic-slice_bitcast_fusion.2, f32[1,16,128]{2,0,1:T(1,128)S(1)} %bitcast.137, f32[3,16,128]{2,0,1:T(4,128)S(1)} %get-tuple-element.481, f32[4,128]{1,0:T(4,128)S(1)} %get-tuple-element.510), kind=kOutput, calls=%fused_computation.6.clone.1 | convolution fusion | flops 14426112 | bytes 632832 | tf_op jit(solution)/shard_map/while/body/while/body/eval_jaxpr/cij,cw->ijw/dot_general | solution.py:33
  65.1 1.8 %multiply_convert_fusion.8 = bf16[16,128,128]{2,1,0:T(8,128)(2,1)S(1)} fusion(f32[128,128]{1,0:T(8,128)S(1)} %get-tuple-element.507, f32[16,128]{1,0:T(8,128)S(1)} %dynamic-slice_bitcast_fusion.2, f32[1,16,128]{2,0,1:T(1,128)S(1)} %bitcast.137, f32[3,16,128]{2,0,1:T(4,128)S(1)} %get-tuple-element.481, f32[4,128]{1,0:T(4,128)S(1)} %get-tuple-element.510), kind=kOutput, calls=%fused_computation.6.clone.1 | convolution fusion | flops 14426112 | bytes 632832 | tf_op jit(solution)/shard_map/while/body/while/body/eval_jaxpr/cij,cw->ijw/dot_general | solution.py:33
  68.3 1.8 %multiply_convert_fusion.8 = bf16[16,128,128]{2,1,0:T(8,128)(2,1)S(1)} fusion(f32[128,128]{1,0:T(8,128)S(1)} %get-tuple-element.507, f32[16,128]{1,0:T(8,128)S(1)} %dynamic-slice_bitcast_fusion.2, f32[1,16,128]{2,0,1:T(1,128)S(1)} %bitcast.137, f32[3,16,128]{2,0,1:T(4,128)S(1)} %get-tuple-element.481, f32[4,128]{1,0:T(4,128)S(1)} %get-tuple-element.510), kind=kOutput, calls=%fused_computation.6.clone.1 | convolution fusion | flops 14426112 | bytes 632832 | tf_op jit(solution)/shard_map/while/body/while/body/eval_jaxpr/cij,cw->ijw/dot_general | solution.py:33
  71.5 1.8 %multiply_convert_fusion.8 = bf16[16,128,128]{2,1,0:T(8,128)(2,1)S(1)} fusion(f32[128,128]{1,0:T(8,128)S(1)} %get-tuple-element.507, f32[16,128]{1,0:T(8,128)S(1)} %dynamic-slice_bitcast_fusion.2, f32[1,16,128]{2,0,1:T(1,128)S(1)} %bitcast.137, f32[3,16,128]{2,0,1:T(4,128)S(1)} %get-tuple-element.481, f32[4,128]{1,0:T(4,128)S(1)} %get-tuple-element.510), kind=kOutput, calls=%fused_computation.6.clone.1 | convolution fusion | flops 14426112 | bytes 632832 | tf_op jit(solution)/shard_map/while/body/while/body/eval_jaxpr/cij,cw->ijw/dot_general | solution.py:33
  74.7 1.8 %multiply_convert_fusion.8 = bf16[16,128,128]{2,1,0:T(8,128)(2,1)S(1)} fusion(f32[128,128]{1,0:T(8,128)S(1)} %get-tuple-element.507, f32[16,128]{1,0:T(8,128)S(1)} %dynamic-slice_bitcast_fusion.2, f32[1,16,128]{2,0,1:T(1,128)S(1)} %bitcast.137, f32[3,16,128]{2,0,1:T(4,128)S(1)} %get-tuple-element.481, f32[4,128]{1,0:T(4,128)S(1)} %get-tuple-element.510), kind=kOutput, calls=%fused_computation.6.clone.1 | convolution fusion | flops 14426112 | bytes 632832 | tf_op jit(solution)/shard_map/while/body/while/body/eval_jaxpr/cij,cw->ijw/dot_general | solution.py:33
  77.9 1.8 %multiply_convert_fusion.8 = bf16[16,128,128]{2,1,0:T(8,128)(2,1)S(1)} fusion(f32[128,128]{1,0:T(8,128)S(1)} %get-tuple-element.507, f32[16,128]{1,0:T(8,128)S(1)} %dynamic-slice_bitcast_fusion.2, f32[1,16,128]{2,0,1:T(1,128)S(1)} %bitcast.137, f32[3,16,128]{2,0,1:T(4,128)S(1)} %get-tuple-element.481, f32[4,128]{1,0:T(4,128)S(1)} %get-tuple-element.510), kind=kOutput, calls=%fused_computation.6.clone.1 | convolution fusion | flops 14426112 | bytes 632832 | tf_op jit(solution)/shard_map/while/body/while/body/eval_jaxpr/cij,cw->ijw/dot_general | solution.py:33
  81.1 1.8 %multiply_convert_fusion.8 = bf16[16,128,128]{2,1,0:T(8,128)(2,1)S(1)} fusion(f32[128,128]{1,0:T(8,128)S(1)} %get-tuple-element.507, f32[16,128]{1,0:T(8,128)S(1)} %dynamic-slice_bitcast_fusion.2, f32[1,16,128]{2,0,1:T(1,128)S(1)} %bitcast.137, f32[3,16,128]{2,0,1:T(4,128)S(1)} %get-tuple-element.481, f32[4,128]{1,0:T(4,128)S(1)} %get-tuple-element.510), kind=kOutput, calls=%fused_computation.6.clone.1 | convolution fusion | flops 14426112 | bytes 632832 | tf_op jit(solution)/shard_map/while/body/while/body/eval_jaxpr/cij,cw->ijw/dot_general | solution.py:33
  84.3 1.8 %multiply_convert_fusion.8 = bf16[16,128,128]{2,1,0:T(8,128)(2,1)S(1)} fusion(f32[128,128]{1,0:T(8,128)S(1)} %get-tuple-element.507, f32[16,128]{1,0:T(8,128)S(1)} %dynamic-slice_bitcast_fusion.2, f32[1,16,128]{2,0,1:T(1,128)S(1)} %bitcast.137, f32[3,16,128]{2,0,1:T(4,128)S(1)} %get-tuple-element.481, f32[4,128]{1,0:T(4,128)S(1)} %get-tuple-element.510), kind=kOutput, calls=%fused_computation.6.clone.1 | convolution fusion | flops 14426112 | bytes 632832 | tf_op jit(solution)/shard_map/while/body/while/body/eval_jaxpr/cij,cw->ijw/dot_general | solution.py:33
  90.0 25.6 %while.24 = (s32[]{:T(128)}, f32[8,16,128]{2,1,0:T(8,128)S(1)}, f32[8,16,128]{2,1,0:T(8,128)S(1)}, f32[128,128]{1,0:T(8,128)S(1)}, f32[3,128]{1,0:T(4,128)S(1)},...) while((s32[]{:T(128)}, f32[8,16,128]{2,1,0:T(8,128)S(1)}, ...), condition=%wide.region_3.3_spmd, body=%wide.region_1.2_spmd.sunk | while | flops 86009856 | bytes 3381177 | solution.py:47
  90.2 1.8 %multiply_convert_fusion.8 = bf16[16,128,128]{2,1,0:T(8,128)(2,1)S(1)} fusion(f32[128,128]{1,0:T(8,128)S(1)} %get-tuple-element.507, f32[16,128]{1,0:T(8,128)S(1)} %dynamic-slice_bitcast_fusion.2, f32[1,16,128]{2,0,1:T(1,128)S(1)} %bitcast.137, f32[3,16,128]{2,0,1:T(4,128)S(1)} %get-tuple-element.481, f32[4,128]{1,0:T(4,128)S(1)} %get-tuple-element.510), kind=kOutput, calls=%fused_computation.6.clone.1 | convolution fusion | flops 14426112 | bytes 632832 | tf_op jit(solution)/shard_map/while/body/while/body/eval_jaxpr/cij,cw->ijw/dot_general | solution.py:33
  93.4 1.8 %multiply_convert_fusion.8 = bf16[16,128,128]{2,1,0:T(8,128)(2,1)S(1)} fusion(f32[128,128]{1,0:T(8,128)S(1)} %get-tuple-element.507, f32[16,128]{1,0:T(8,128)S(1)} %dynamic-slice_bitcast_fusion.2, f32[1,16,128]{2,0,1:T(1,128)S(1)} %bitcast.137, f32[3,16,128]{2,0,1:T(4,128)S(1)} %get-tuple-element.481, f32[4,128]{1,0:T(4,128)S(1)} %get-tuple-element.510), kind=kOutput, calls=%fused_computation.6.clone.1 | convolution fusion | flops 14426112 | bytes 632832 | tf_op jit(solution)/shard_map/while/body/while/body/eval_jaxpr/cij,cw->ijw/dot_general | solution.py:33
  96.6 1.8 %multiply_convert_fusion.8 = bf16[16,128,128]{2,1,0:T(8,128)(2,1)S(1)} fusion(f32[128,128]{1,0:T(8,128)S(1)} %get-tuple-element.507, f32[16,128]{1,0:T(8,128)S(1)} %dynamic-slice_bitcast_fusion.2, f32[1,16,128]{2,0,1:T(1,128)S(1)} %bitcast.137, f32[3,16,128]{2,0,1:T(4,128)S(1)} %get-tuple-element.481, f32[4,128]{1,0:T(4,128)S(1)} %get-tuple-element.510), kind=kOutput, calls=%fused_computation.6.clone.1 | convolution fusion | flops 14426112 | bytes 632832 | tf_op jit(solution)/shard_map/while/body/while/body/eval_jaxpr/cij,cw->ijw/dot_general | solution.py:33
  99.8 1.8 %multiply_convert_fusion.8 = bf16[16,128,128]{2,1,0:T(8,128)(2,1)S(1)} fusion(f32[128,128]{1,0:T(8,128)S(1)} %get-tuple-element.507, f32[16,128]{1,0:T(8,128)S(1)} %dynamic-slice_bitcast_fusion.2, f32[1,16,128]{2,0,1:T(1,128)S(1)} %bitcast.137, f32[3,16,128]{2,0,1:T(4,128)S(1)} %get-tuple-element.481, f32[4,128]{1,0:T(4,128)S(1)} %get-tuple-element.510), kind=kOutput, calls=%fused_computation.6.clone.1 | convolution fusion | flops 14426112 | bytes 632832 | tf_op jit(solution)/shard_map/while/body/while/body/eval_jaxpr/cij,cw->ijw/dot_general | solution.py:33
  103.0 1.8 %multiply_convert_fusion.8 = bf16[16,128,128]{2,1,0:T(8,128)(2,1)S(1)} fusion(f32[128,128]{1,0:T(8,128)S(1)} %get-tuple-element.507, f32[16,128]{1,0:T(8,128)S(1)} %dynamic-slice_bitcast_fusion.2, f32[1,16,128]{2,0,1:T(1,128)S(1)} %bitcast.137, f32[3,16,128]{2,0,1:T(4,128)S(1)} %get-tuple-element.481, f32[4,128]{1,0:T(4,128)S(1)} %get-tuple-element.510), kind=kOutput, calls=%fused_computation.6.clone.1 | convolution fusion | flops 14426112 | bytes 632832 | tf_op jit(solution)/shard_map/while/body/while/body/eval_jaxpr/cij,cw->ijw/dot_general | solution.py:33
  106.2 1.8 %multiply_convert_fusion.8 = bf16[16,128,128]{2,1,0:T(8,128)(2,1)S(1)} fusion(f32[128,128]{1,0:T(8,128)S(1)} %get-tuple-element.507, f32[16,128]{1,0:T(8,128)S(1)} %dynamic-slice_bitcast_fusion.2, f32[1,16,128]{2,0,1:T(1,128)S(1)} %bitcast.137, f32[3,16,128]{2,0,1:T(4,128)S(1)} %get-tuple-element.481, f32[4,128]{1,0:T(4,128)S(1)} %get-tuple-element.510), kind=kOutput, calls=%fused_computation.6.clone.1 | convolution fusion | flops 14426112 | bytes 632832 | tf_op jit(solution)/shard_map/while/body/while/body/eval_jaxpr/cij,cw->ijw/dot_general | solution.py:33
  109.4 1.8 %multiply_convert_fusion.8 = bf16[16,128,128]{2,1,0:T(8,128)(2,1)S(1)} fusion(f32[128,128]{1,0:T(8,128)S(1)} %get-tuple-element.507, f32[16,128]{1,0:T(8,128)S(1)} %dynamic-slice_bitcast_fusion.2, f32[1,16,128]{2,0,1:T(1,128)S(1)} %bitcast.137, f32[3,16,128]{2,0,1:T(4,128)S(1)} %get-tuple-element.481, f32[4,128]{1,0:T(4,128)S(1)} %get-tuple-element.510), kind=kOutput, calls=%fused_computation.6.clone.1 | convolution fusion | flops 14426112 | bytes 632832 | tf_op jit(solution)/shard_map/while/body/while/body/eval_jaxpr/cij,cw->ijw/dot_general | solution.py:33
  (311 shorter events, 51.6 us)
Async XLA Ops:
  0.0 115.6 %copy-start = (bf16[1,128,128]{2,1,0:T(8,128)(2,1)S(1)}, bf16[1,128,128]{2,1,0:T(8,128)(2,1)}, u32[]{:S(2)}) copy-start(bf16[1,128,128]{2,1,0:T(8,128)(2,1)} %param.30) | copy-start | bytes 98308
  5.9 7.4 %copy-start.6 = (bf16[1,1,1,3,128]{4,3,2,1,0:T(4,128)(2,1)S(1)}, bf16[1,1,1,3,128]{4,3,2,1,0:T(4,128)(2,1)}, u32[]{:S(2)}) copy-start(bf16[1,1,1,3,128]{4,3,2,1,0:T(4,128)(2,1)} %param.19) | copy-start | bytes 2308
  5.9 19.3 %copy-start.5 = (s32[1,1,1,384]{3,2,1,0:T(1,128)S(1)}, s32[1,1,1,384]{3,2,1,0:T(1,128)}, u32[]{:S(2)}) copy-start(s32[1,1,1,384]{3,2,1,0:T(1,128)} %param.20) | copy-start | bytes 4612
  5.9 20.1 %copy-start.3 = (bf16[1,128,128]{2,1,0:T(8,128)(2,1)S(1)}, bf16[1,128,128]{2,1,0:T(8,128)(2,1)}, u32[]{:S(2)}) copy-start(bf16[1,128,128]{2,1,0:T(8,128)(2,1)} %param.28) | copy-start | bytes 98308
  7.9 18.1 %copy-start.2 = (bf16[1,1,1,128,128]{4,3,2,1,0:T(8,128)(2,1)S(1)}, bf16[1,1,1,128,128]{4,3,2,1,0:T(8,128)(2,1)}, u32[]{:S(2)}) copy-start(bf16[1,1,1,128,128]{4,3,2,1,0:T(8,128)(2,1)} %param.18) | copy-start | bytes 98308
  7.9 21.8 %collective-permute-start.2 = (bf16[1,2,2,128,128]{4,3,2,1,0:T(8,128)(2,1)S(1)}, bf16[1,2,2,128,128]{4,3,2,1,0:T(8,128)(2,1)S(1)}, u32[]{:S(2)}, u32[]{:S(2)}) collective-permute-start(bf16[1,2,2,128,128]{4,3,2,1,0:T(8,128)(2,1)S(1)} %bitcast.141), channel_id=1, source_target_pairs={{0,4},{4,8},{8,12},{1,5},{5,9},{9,13},{2,6},{6,10},{10,14},{3,7},{... | collective-permute-start | bytes 393224 | tf_op jit(solution)/shard_map/ppermute | solution.py:16
  12.0 17.7 %collective-permute-start.3 = (bf16[1,2,2,128,128]{4,3,2,1,0:T(8,128)(2,1)S(1)}, bf16[1,2,2,128,128]{4,3,2,1,0:T(8,128)(2,1)S(1)}, u32[]{:S(2)}, u32[]{:S(2)}) collective-permute-start(bf16[1,2,2,128,128]{4,3,2,1,0:T(8,128)(2,1)S(1)} %bitcast.142), channel_id=1, source_target_pairs={{4,0},{8,4},{12,8},{5,1},{9,5},{13,9},{6,2},{10,6},{14,10},{7,3},{... | collective-permute-start | bytes 393224 | tf_op jit(solution)/shard_map/ppermute | solution.py:17
  19.4 8.5 %collective-permute-start = (bf16[1,2,2,3,128]{4,3,2,1,0:T(4,128)(2,1)S(1)}, bf16[1,2,2,3,128]{4,3,2,1,0:T(4,128)(2,1)S(1)}, u32[]{:S(2)}, u32[]{:S(2)}) collective-permute-start(bf16[1,2,2,3,128]{4,3,2,1,0:T(4,128)(2,1)S(1)} %bitcast.145), channel_id=1, source_target_pairs={{0,4},{4,8},{8,12},{1,5},{5,9},{9,13},{2,6},{6,10},{10,14},{3,7},{... | collective-permute-start | bytes 9224 | tf_op jit(solution)/shard_map/ppermute | solution.py:16
  23.9 5.5 %collective-permute-start.1 = (bf16[1,2,2,3,128]{4,3,2,1,0:T(4,128)(2,1)S(1)}, bf16[1,2,2,3,128]{4,3,2,1,0:T(4,128)(2,1)S(1)}, u32[]{:S(2)}, u32[]{:S(2)}) collective-permute-start(bf16[1,2,2,3,128]{4,3,2,1,0:T(4,128)(2,1)S(1)} %bitcast.146), channel_id=1, source_target_pairs={{4,0},{8,4},{12,8},{5,1},{9,5},{13,9},{6,2},{10,6},{14,10},{7,3},{... | collective-permute-start | bytes 9224 | tf_op jit(solution)/shard_map/ppermute | solution.py:17
  25.4 0.7 copy-start.7
  26.1 0.8 copy-start.4
  26.2 0.7 copy-start.8
  29.8 0.8 copy-start.1
  29.8 0.8 copy-start.10
  29.8 0.8 copy-start.12
  30.6 85.0 %copy-start.11 = (bf16[1,128,128]{2,1,0:T(8,128)(2,1)S(1)}, bf16[1,128,128]{2,1,0:T(8,128)(2,1)}, u32[]{:S(2)}) copy-start(bf16[1,128,128]{2,1,0:T(8,128)(2,1)} %param.29) | copy-start | bytes 98308
  116.0 0.7 copy-start.9
